TPU v7x, 128 devices: a whole 4x4x4 slice. The times are simulated.
128 devices in a mesh: gx: 16 (over x_hi, z, core), gy: 8 (over y, x_lo).
Axes of the slice: x: 4 (x_hi: 2, x_lo: 2; x = x_hi * 2 + x_lo), y: 4, z: 4, core: 2. Of those that a mesh axis runs over, the one named last changes fastest.
Arguments:
- signal: float32 [131072, 128], P(('gx', 'gy')), may hold values from -6 to 6
- filter_taps: float32 [131072, 128], P(('gx', 'gy')), may hold values from -6 to 6
- grad_out: float32 [131072, 128], P(('gx', 'gy')), may hold values from -0.015625 to 0.015625
Outputs:
- grad_signal: float32 [131072, 128], P(('gx', 'gy'))
- grad_filter: float32 [131072, 128], P(('gx', 'gy'))
All inputs are finite; a program needn't handle non-finite values.
Results may differ from a plain program's by a relative error of at most 0.000098.
Values sent between devices are 32-bit elements; how exact they have to be, the bound alone decides.
No kernel may reach another device: no remote copies, remote signals or barrier semaphores. Data moves between devices by JAX's collectives and lax.ppermute only.
A program may use at most 128 MiB of HBM per device.

v0:
```python
import jax
import jax.numpy as jnp
import numpy as np
from jax import lax
from jax.experimental import pallas as pl
from jax.experimental.pallas import tpu as pltpu
from jax.sharding import PartitionSpec as P

f32 = jnp.float32
bf16 = jnp.bfloat16
AXES = ("gx", "gy")
B = 128
RADIX = 8


def turn(count):
    angle = 2.0 * np.pi * count
    return np.cos(angle), np.sin(angle)


def halves(matrix):
    high = matrix.astype(np.float32).astype(jnp.bfloat16)
    low = (matrix - high.astype(np.float64)).astype(np.float32).astype(jnp.bfloat16)
    return high, low


def tables(length):
    index = np.arange(B)
    cosine, sine = turn((index[:, None] * index[None, :] % B) / B)
    left = np.block([[cosine, sine], [-sine, cosine]])
    left_back = np.block([[cosine, -sine], [sine, cosine]])
    packed = []
    for matrix in (left, left_back):
        high, low = halves(matrix)
        packed.append(np.concatenate([high, high, low], axis=1))
    for matrix in (left.T, left_back.T):
        high, low = halves(matrix)
        packed.append(np.concatenate([high, low], axis=0))
    m = np.arange(RADIX)
    inner = index[None, :, None] * (m[:, None, None] + 0.25) / (RADIX * B) * np.ones((1, 1, B))
    inner = np.stack(turn(inner), axis=1)
    outer = index[None, None, :] * (RADIX * index[None, :, None] + m[:, None, None] + 0.25) / length
    outer = np.stack(turn(outer), axis=1)
    return packed, inner.astype(np.float32), outer.astype(np.float32)


def scaled(pair, constant):
    real, imaginary = pair
    cosine, sine = constant
    return real * cosine - imaginary * sine, real * sine + imaginary * cosine


def spread(rows):
    root = np.float32(np.sqrt(0.5))
    out = [None] * RADIX
    halfway = [rows[a + 4] * root for a in range(4)]
    for odd in range(2):
        points = []
        for a in range(4):
            if odd:
                pair = (rows[a] - halfway[a], halfway[a])
            else:
                pair = (rows[a] + halfway[a], -halfway[a])
            if a:
                cosine, sine = turn(-a * (odd + 0.25) / RADIX)
                pair = scaled(pair, (np.float32(cosine), np.float32(sine)))
            points.append(pair)
        (r0, i0), (r1, i1), (r2, i2), (r3, i3) = points
        er, ei, fr, fi = r0 + r2, i0 + i2, r0 - r2, i0 - i2
        gr, gi, hr, hi = r1 + r3, i1 + i3, r1 - r3, i1 - i3
        out[odd] = (er + gr, ei + gi)
        out[2 + odd] = (fr + hi, fi - hr)
        out[4 + odd] = (er - gr, ei - gi)
        out[6 + odd] = (fr - hi, fi + hr)
    return out


def gather_real(parts):
    root = np.float32(np.sqrt(0.5))
    rows = [None] * RADIX
    both = []
    for odd in range(2):
        (r0, i0), (r1, i1), (r2, i2), (r3, i3) = (parts[2 * n + odd] for n in range(4))
        er, ei, fr, fi = r0 + r2, i0 + i2, r0 - r2, i0 - i2
        gr, gi, hr, hi = r1 + r3, i1 + i3, r1 - r3, i1 - i3
        points = [(er + gr, ei + gi), (fr - hi, fi + hr), (er - gr, ei - gi), (fr + hi, fi - hr)]
        for a in range(1, 4):
            cosine, sine = turn(a * (odd + 0.25) / RADIX)
            points[a] = scaled(points[a], (np.float32(cosine), np.float32(sine)))
        both.append(points)
    for a in range(4):
        (er, ei), (fr, fi) = both[0][a], both[1][a]
        rows[a] = er + fr
        rows[a + 4] = ((er - fr) - (ei - fi)) * root
    return rows


def split(value):
    high = value.astype(bf16)
    return high, (value - high.astype(f32)).astype(bf16)


def times(pattern, left, right):
    return jnp.dot(left, right, preferred_element_type=f32)


def left_product(matrix_ref, data):
    return jnp.dot(matrix_ref[:, : 4 * B], data, preferred_element_type=f32) + jnp.dot(
        matrix_ref[:, 4 * B :], data[: 2 * B], preferred_element_type=f32
    )


def right_product(high, low, matrix_ref):
    top = matrix_ref[: 2 * B, :]
    return (
        jnp.dot(high, top, preferred_element_type=f32)
        + jnp.dot(low, top, preferred_element_type=f32)
        + jnp.dot(high, matrix_ref[2 * B :, :], preferred_element_type=f32)
    )


def pack_kernel(signal_ref, filter_ref, grad_ref, out_ref):
    for q, ref in enumerate((signal_ref, filter_ref, grad_ref)):
        for r in range(ref.shape[0] // B):
            out_ref[:, 8 * q + r, :] = ref[r * B : (r + 1) * B, :].T


def unpack_kernel(in_ref, first_ref, second_ref):
    for q, ref in enumerate((first_ref, second_ref)):
        for r in range(ref.shape[0] // B):
            ref[r * B : (r + 1) * B, :] = in_ref[:, 8 * q + r, :].T


CHUNK = 16


def channel_kernel(scale, in_ref, left_ref, left_back_ref, right_ref, right_back_ref, inner_ref, outer_ref, out_ref, stage, back):
    blocks = in_ref.shape[0] // RADIX
    for q in range(3):
        for chunk in range(B // CHUNK):
            rows = []
            for a in range(RADIX):
                start = a * blocks + chunk * (CHUNK // 8)
                rows.append(in_ref[start : start + CHUNK // 8, 8 * q : 8 * q + 8, :].reshape(CHUNK, B))
            here = slice(chunk * CHUNK, (chunk + 1) * CHUNK)
            for m, pair in enumerate(spread(rows)):
                real, imaginary = scaled(pair, (inner_ref[m, 0, here, :], -inner_ref[m, 1, here, :]))
                lanes = slice((m % 2) * B, (m % 2 + 1) * B)
                for part, value in enumerate((real, imaginary)):
                    high, low = split(value)
                    at = part * B + chunk * CHUNK
                    stage[q, m // 2, at : at + CHUNK, lanes] = high
                    stage[q, m // 2, 2 * B + at : 2 * B + at + CHUNK, lanes] = low
    for pair_at in range(RADIX // 2):
        spectra = []
        for q in range(3):
            mixed = left_product(left_ref, stage[q, pair_at])
            turned = []
            for half in range(2):
                m = 2 * pair_at + half
                lanes = slice(half * B, (half + 1) * B)
                real, imaginary = scaled(
                    (mixed[:B, lanes], mixed[B:, lanes]), (outer_ref[m, 0], -outer_ref[m, 1])
                )
                turned.append(jnp.concatenate([real, imaginary], axis=1))
            high, low = split(jnp.concatenate(turned, axis=0))
            spectra.append(right_product(high, low, right_ref))
        grad_re, grad_im = spectra[2][:, :B], spectra[2][:, B:]
        for q in range(2):
            other_re, other_im = spectra[1 - q][:, :B], spectra[1 - q][:, B:]
            product = jnp.concatenate(
                [other_re * grad_re + other_im * grad_im, other_re * grad_im - other_im * grad_re], axis=1
            )
            high, low = split(product)
            mixed = right_product(high, low, right_back_ref)
            columns = []
            for half in range(2):
                m = 2 * pair_at + half
                real, imaginary = scaled(
                    (mixed[half * B : (half + 1) * B, :B], mixed[half * B : (half + 1) * B, B:]),
                    (outer_ref[m, 0], outer_ref[m, 1]),
                )
                columns.append(jnp.concatenate([real, imaginary], axis=0))
            high, low = split(jnp.concatenate(columns, axis=1))
            back[q, pair_at] = left_product(left_back_ref, jnp.concatenate([high, low], axis=0))
    for q in range(2):
        for chunk in range(B // CHUNK):
            here = slice(chunk * CHUNK, (chunk + 1) * CHUNK)
            parts = []
            for m in range(RADIX):
                lanes = slice((m % 2) * B, (m % 2 + 1) * B)
                at = chunk * CHUNK
                pair = (back[q, m // 2, at : at + CHUNK, lanes], back[q, m // 2, B + at : B + at + CHUNK, lanes])
                parts.append(scaled(pair, (inner_ref[m, 0, here, :], inner_ref[m, 1, here, :])))
            for a, row in enumerate(gather_real(parts)):
                start = a * blocks + chunk * (CHUNK // 8)
                out_ref[start : start + CHUNK // 8, 8 * q : 8 * q + 8, :] = (row * scale).reshape(CHUNK // 8, 8, B)


def whole(count):
    return [pl.BlockSpec(memory_space=pltpu.VMEM)] * count


def call(kernel, outs, count, name, scratch=(), interpret=False):
    specs = whole(len(outs))
    return pl.pallas_call(
        kernel,
        out_shape=outs,
        in_specs=whole(count),
        out_specs=specs,
        scratch_shapes=list(scratch),
        name=name,
        interpret=interpret,
        compiler_params=pltpu.CompilerParams(vmem_limit_bytes=48 * 1024 * 1024),
    )


def pack(signal, filter_taps, grad_out, interpret=False):
    shape = jax.ShapeDtypeStruct((B, 24, B), f32)
    return call(pack_kernel, [shape], 3, "pack", interpret=interpret)(signal, filter_taps, grad_out)[0]


def transform(received, interpret=False):
    blocks = received.shape[0]
    length = blocks * 8 * B
    packed, inner, outer = tables(length)
    constants = [jnp.asarray(table) for table in packed] + [jnp.asarray(inner), jnp.asarray(outer)]

    def kernel(*refs):
        channel_kernel(np.float32(1.0 / length), *refs)

    shape = jax.ShapeDtypeStruct((blocks, 16, B), f32)
    scratch = [pltpu.VMEM((3, RADIX // 2, 4 * B, 2 * B), bf16), pltpu.VMEM((2, RADIX // 2, 2 * B, 2 * B), f32)]
    return call(kernel, [shape], 7, "channel", scratch, interpret)(received, *constants)[0]


def unpack(received, interpret=False):
    shape = jax.ShapeDtypeStruct((8 * B, B), f32)
    return call(unpack_kernel, [shape, shape], 1, "unpack", interpret=interpret)(received)


def exchange(array):
    return lax.all_to_all(array, AXES, split_axis=0, concat_axis=0, tiled=True)


def shards(signal, filter_taps, grad_out):
    received = exchange(pack(signal, filter_taps, grad_out))
    returned = exchange(transform(received))
    first, second = unpack(returned)
    return first, second


def solution(mesh):
    return jax.shard_map(
        shards,
        mesh=mesh,
        in_specs=(P(AXES, None), P(AXES, None), P(AXES, None)),
        out_specs=(P(AXES, None), P(AXES, None)),
        check_vma=False,
    )
```

profile of v0, /device:TPU:0, one launch (start us, length us, event | category | flops | bytes accessed | tf_op | source)
XLA Modules:
  0.0 72.4 jit_solution(13869878344739076395)
XLA Ops:
  0.6 0.0 copy-start.2
  0.6 1.0 %copy-done.2 = f32[1024,128]{1,0:T(8,128)S(1)} copy-done((f32[1024,128]{1,0:T(8,128)S(1)}, f32[1024,128]{1,0:T(8,128)}, u32[]{:S(2)}) %copy-start.2) | copy-done | bytes 524312
  1.7 0.0 copy-start.3
  1.7 1.0 %copy-done.3 = f32[1024,128]{1,0:T(8,128)S(1)} copy-done((f32[1024,128]{1,0:T(8,128)S(1)}, f32[1024,128]{1,0:T(8,128)}, u32[]{:S(2)}) %copy-start.3) | copy-done | bytes 524312
  2.7 0.0 copy-start.4
  2.7 1.0 %copy-done.4 = f32[1024,128]{1,0:T(8,128)S(1)} copy-done((f32[1024,128]{1,0:T(8,128)S(1)}, f32[1024,128]{1,0:T(8,128)}, u32[]{:S(2)}) %copy-start.4) | copy-done | bytes 524312
  3.8 0.0 copy-start.8
  3.8 0.9 %pack.1 = f32[128,24,128]{2,1,0:T(8,128)S(1)} custom-call(f32[1024,128]{1,0:T(8,128)S(1)} %copy-done.2, f32[1024,128]{1,0:T(8,128)S(1)} %copy-done.3, f32[1024,128]{1,0:T(8,128)S(1)} %copy-done.4), custom_call_target="tpu_custom_call" | custom-call | tf_op jit(solution)/shard_map/pack/pallas_call | solution.py:220
  4.7 0.0 copy-start
  4.7 0.0 copy-start.1
  4.7 0.0 copy-start.5
  4.7 0.0 copy-start.6
  4.7 0.0 copy-start.7
  4.8 35.4 %all_to_all.10.refs_0_ = f32[128,24,128]{2,1,0:T(8,128)S(1)} all-to-all(f32[128,24,128]{2,1,0:T(8,128)S(1)} %pack.1), channel_id=1, replica_groups=mesh['gx'=16,'gy'=8] {'gx','gy'}, dimensions={0} | all-to-all | bytes 3145728 | tf_op jit(solution)/shard_map/all_to_all | solution.py:243
  40.1 0.0 copy-done.8
  40.1 0.0 copy-done
  40.1 0.0 copy-done.1
  40.1 0.0 copy-done.5
  40.1 0.0 copy-done.6
  40.2 0.0 copy-done.7
  40.2 7.6 %channel.1 = f32[128,16,128]{2,1,0:T(8,128)S(1)} custom-call(f32[128,24,128]{2,1,0:T(8,128)S(1)} %all_to_all.10.refs_0_, bf16[256,768]{1,0:T(8,128)(2,1)S(1)} %copy-done.6, bf16[256,768]{1,0:T(8,128)(2,1)S(1)} %copy-done.5, bf16[512,256]{1,0:T(8,128)(2,1)S(1)} %copy-done.8, bf16[512,256]{1,0:T(8,128)(2,1)S(1)} %copy-done.7, ...), custom_call_target="tpu_custom_call" | custom-call | tf_op jit(solution)/shard_map/channel/pallas_call | solution.py:234
  47.7 23.1 %all_to_all.11.in_ref = f32[128,16,128]{2,1,0:T(8,128)S(1)} all-to-all(f32[128,16,128]{2,1,0:T(8,128)S(1)} %channel.1), channel_id=1, replica_groups=mesh['gx'=16,'gy'=8] {'gx','gy'}, dimensions={0} | all-to-all | bytes 2097152 | tf_op jit(solution)/shard_map/all_to_all | solution.py:243
  70.9 1.5 %unpack.1 = (f32[1024,128]{1,0:T(8,128)}, f32[1024,128]{1,0:T(8,128)}) custom-call(f32[128,16,128]{2,1,0:T(8,128)S(1)} %all_to_all.11.in_ref), custom_call_target="tpu_custom_call" | custom-call | tf_op jit(solution)/shard_map/unpack/pallas_call | solution.py:239
Async XLA Ops:
  0.6 1.0 %copy-start.2 = (f32[1024,128]{1,0:T(8,128)S(1)}, f32[1024,128]{1,0:T(8,128)}, u32[]{:S(2)}) copy-start(f32[1024,128]{1,0:T(8,128)} %signal_ref.1) | copy-start | bytes 1572868
  1.7 1.0 %copy-start.3 = (f32[1024,128]{1,0:T(8,128)S(1)}, f32[1024,128]{1,0:T(8,128)}, u32[]{:S(2)}) copy-start(f32[1024,128]{1,0:T(8,128)} %filter_ref.1) | copy-start | bytes 1572868
  2.7 1.0 %copy-start.4 = (f32[1024,128]{1,0:T(8,128)S(1)}, f32[1024,128]{1,0:T(8,128)}, u32[]{:S(2)}) copy-start(f32[1024,128]{1,0:T(8,128)} %grad_ref.1) | copy-start | bytes 1572868
  3.8 36.4 %copy-start.8 = (bf16[512,256]{1,0:T(8,128)(2,1)S(1)}, bf16[512,256]{1,0:T(8,128)(2,1)}, u32[]{:S(2)}) copy-start(bf16[512,256]{1,0:T(8,128)(2,1)} %constant.14.clone.refs_3_) | copy-start | bytes 786436
  4.7 35.4 %copy-start = (f32[8,2,128,128]{3,2,1,0:T(8,128)S(1)}, f32[8,2,128,128]{3,2,1,0:T(8,128)}, u32[]{:S(2)}) copy-start(f32[8,2,128,128]{3,2,1,0:T(8,128)} %constant.17.clone.refs_6_) | copy-start | bytes 3145732
  4.7 35.4 %copy-start.1 = (f32[8,2,128,128]{3,2,1,0:T(8,128)S(1)}, f32[8,2,128,128]{3,2,1,0:T(8,128)}, u32[]{:S(2)}) copy-start(f32[8,2,128,128]{3,2,1,0:T(8,128)} %constant.16.clone.refs_5_) | copy-start | bytes 3145732
  4.7 35.4 %copy-start.5 = (bf16[256,768]{1,0:T(8,128)(2,1)S(1)}, bf16[256,768]{1,0:T(8,128)(2,1)}, u32[]{:S(2)}) copy-start(bf16[256,768]{1,0:T(8,128)(2,1)} %constant.13.clone.refs_2_) | copy-start | bytes 1179652
  4.7 35.4 %copy-start.6 = (bf16[256,768]{1,0:T(8,128)(2,1)S(1)}, bf16[256,768]{1,0:T(8,128)(2,1)}, u32[]{:S(2)}) copy-start(bf16[256,768]{1,0:T(8,128)(2,1)} %constant.12.clone.refs_1_) | copy-start | bytes 1179652
  4.7 35.4 %copy-start.7 = (bf16[512,256]{1,0:T(8,128)(2,1)S(1)}, bf16[512,256]{1,0:T(8,128)(2,1)}, u32[]{:S(2)}) copy-start(bf16[512,256]{1,0:T(8,128)(2,1)} %constant.15.clone.refs_4_) | copy-start | bytes 786436
where the time goes:
time: 72.7 us; the launch traced here: 72.4 us
  blocking collectives  58.5 us (80%)
  Pallas kernels  10 us (14%)
  local copies, waits for them, and re-layouts  3.15 us (4%)
  between operations  0.73 us (1%)
    all_to_all x2, blocking collectives, exchange(): return lax.all_to_all(array, AXES, split_axis=0, concat_axis=0, tiled=True)  58.5 us
    pallas_call x1, Pallas kernels, transform(): call(kernel, [shape], 7, 'channel', scratch, interpret)  7.57 us
    unnamed x18, local copies, waits for them, and re-layouts  3.15 us
    pallas_call x1, Pallas kernels, unpack(): call(unpack_kernel, [shape, shape], 1, 'unpack', interpret=interpret)  1.52 us

commit v1 on v0

--- a/solution.py
+++ b/solution.py
@@ -37,10 +37,9 @@
         high, low = halves(matrix)
         packed.append(np.concatenate([high, low], axis=0))
     m = np.arange(RADIX)
-    inner = index[None, :, None] * (m[:, None, None] + 0.25) / (RADIX * B) * np.ones((1, 1, B))
-    inner = np.stack(turn(inner), axis=1)
-    outer = index[None, None, :] * (RADIX * index[None, :, None] + m[:, None, None] + 0.25) / length
-    outer = np.stack(turn(outer), axis=1)
+    position = B * index[:, None] + index[None, :]
+    inner = np.stack(turn(position[None] * (m[:, None, None] + 0.25) / length), axis=1)
+    outer = np.stack(turn(RADIX * index[:, None] * index[None, :] / length))
     return packed, inner.astype(np.float32), outer.astype(np.float32)
 
 
@@ -100,10 +99,6 @@
     return high, (value - high.astype(f32)).astype(bf16)
 
 
-def times(pattern, left, right):
-    return jnp.dot(left, right, preferred_element_type=f32)
-
-
 def left_product(matrix_ref, data):
     return jnp.dot(matrix_ref[:, : 4 * B], data, preferred_element_type=f32) + jnp.dot(
         matrix_ref[:, 4 * B :], data[: 2 * B], preferred_element_type=f32
@@ -119,16 +114,31 @@
     )
 
 
-def pack_kernel(signal_ref, filter_ref, grad_ref, out_ref):
-    for q, ref in enumerate((signal_ref, filter_ref, grad_ref)):
-        for r in range(ref.shape[0] // B):
-            out_ref[:, 8 * q + r, :] = ref[r * B : (r + 1) * B, :].T
-
-
-def unpack_kernel(in_ref, first_ref, second_ref):
+def pack_kernel(signal_ref, filter_ref, grad_ref, out_ref, held, arrived):
+    refs = (signal_ref, filter_ref, grad_ref)
+    rows = signal_ref.shape[0] // B
+    copies = []
+    for r in range(rows):
+        for q, ref in enumerate(refs):
+            here = pl.ds(r * B, B)
+            copies.append(pltpu.make_async_copy(ref.at[here], held.at[q, here], arrived.at[q, r]))
+            copies[-1].start()
+    for r in range(rows):
+        for q in range(3):
+            copies[3 * r + q].wait()
+            out_ref[:, 8 * q + r, :] = held[q, r * B : (r + 1) * B, :].T
+
+
+def unpack_kernel(in_ref, first_ref, second_ref, held, left):
+    copies = []
     for q, ref in enumerate((first_ref, second_ref)):
         for r in range(ref.shape[0] // B):
-            ref[r * B : (r + 1) * B, :] = in_ref[:, 8 * q + r, :].T
+            held[q, r * B : (r + 1) * B, :] = in_ref[:, 8 * q + r, :].T
+            here = pl.ds(r * B, B)
+            copies.append(pltpu.make_async_copy(held.at[q, here], ref.at[here], left.at[q, r]))
+            copies[-1].start()
+    for copy in copies:
+        copy.wait()
 
 
 CHUNK = 16
@@ -160,7 +170,7 @@
                 m = 2 * pair_at + half
                 lanes = slice(half * B, (half + 1) * B)
                 real, imaginary = scaled(
-                    (mixed[:B, lanes], mixed[B:, lanes]), (outer_ref[m, 0], -outer_ref[m, 1])
+                    (mixed[:B, lanes], mixed[B:, lanes]), (outer_ref[0], -outer_ref[1])
                 )
                 turned.append(jnp.concatenate([real, imaginary], axis=1))
             high, low = split(jnp.concatenate(turned, axis=0))
@@ -178,7 +188,7 @@
                 m = 2 * pair_at + half
                 real, imaginary = scaled(
                     (mixed[half * B : (half + 1) * B, :B], mixed[half * B : (half + 1) * B, B:]),
-                    (outer_ref[m, 0], outer_ref[m, 1]),
+                    (outer_ref[0], outer_ref[1]),
                 )
                 columns.append(jnp.concatenate([real, imaginary], axis=0))
             high, low = split(jnp.concatenate(columns, axis=1))
@@ -197,18 +207,13 @@
                 out_ref[start : start + CHUNK // 8, 8 * q : 8 * q + 8, :] = (row * scale).reshape(CHUNK // 8, 8, B)
 
 
-def whole(count):
-    return [pl.BlockSpec(memory_space=pltpu.VMEM)] * count
-
-
-def call(kernel, outs, count, name, scratch=(), interpret=False):
-    specs = whole(len(outs))
+def call(kernel, out_shape, in_spaces, out_spaces, name, scratch, interpret):
     return pl.pallas_call(
         kernel,
-        out_shape=outs,
-        in_specs=whole(count),
-        out_specs=specs,
-        scratch_shapes=list(scratch),
+        out_shape=out_shape,
+        in_specs=[pl.BlockSpec(memory_space=space) for space in in_spaces],
+        out_specs=[pl.BlockSpec(memory_space=space) for space in out_spaces],
+        scratch_shapes=scratch,
         name=name,
         interpret=interpret,
         compiler_params=pltpu.CompilerParams(vmem_limit_bytes=48 * 1024 * 1024),
@@ -216,8 +221,14 @@
 
 
 def pack(signal, filter_taps, grad_out, interpret=False):
+    rows = signal.shape[0]
     shape = jax.ShapeDtypeStruct((B, 24, B), f32)
-    return call(pack_kernel, [shape], 3, "pack", interpret=interpret)(signal, filter_taps, grad_out)[0]
+    scratch = [pltpu.VMEM((3, rows, B), f32), pltpu.SemaphoreType.DMA((3, rows // B))]
+    packed = call(pack_kernel, [shape], [pltpu.HBM] * 3, [pltpu.VMEM], "pack", scratch, interpret)
+    inputs = (signal, filter_taps, grad_out)
+    if not interpret:
+        inputs = [pltpu.with_memory_space_constraint(x, pltpu.HBM) for x in inputs]
+    return packed(*inputs)[0]
 
 
 def transform(received, interpret=False):
@@ -231,12 +242,14 @@
 
     shape = jax.ShapeDtypeStruct((blocks, 16, B), f32)
     scratch = [pltpu.VMEM((3, RADIX // 2, 4 * B, 2 * B), bf16), pltpu.VMEM((2, RADIX // 2, 2 * B, 2 * B), f32)]
-    return call(kernel, [shape], 7, "channel", scratch, interpret)(received, *constants)[0]
+    return call(kernel, [shape], [pltpu.VMEM] * 7, [pltpu.VMEM], "channel", scratch, interpret)(received, *constants)[0]
 
 
 def unpack(received, interpret=False):
-    shape = jax.ShapeDtypeStruct((8 * B, B), f32)
-    return call(unpack_kernel, [shape, shape], 1, "unpack", interpret=interpret)(received)
+    rows = 8 * B
+    shape = jax.ShapeDtypeStruct((rows, B), f32)
+    scratch = [pltpu.VMEM((2, rows, B), f32), pltpu.SemaphoreType.DMA((2, rows // B))]
+    return call(unpack_kernel, [shape] * 2, [pltpu.VMEM], [pltpu.HBM] * 2, "unpack", scratch, interpret)(received)
 
 
 def exchange(array):

time: 72.7 us -> 72.1 us (level)
  local copies, waits for them, and re-layouts: 3.15 us -> 0.04 us
  Pallas kernels: 10 us -> 12.6 us
    unnamed x18 -> x12, local copies, waits for them, and re-layouts: 3.15 us -> 0.04 us
    pallas_call x3, Pallas kernels: 10 us -> 12.6 us  [the longest x1 7.52 us: transform(): call(kernel, [shape], [pltpu.VMEM] * 7, [pltpu.VMEM], 'channel', scratch,...]
where the time goes in v1:
time: 72.1 us; the launch traced here: 71.9 us
  blocking collectives  58.5 us (81%)
  Pallas kernels  12.6 us (17%)
    all_to_all x2, blocking collectives, exchange(): return lax.all_to_all(array, AXES, split_axis=0, concat_axis=0, tiled=True)  58.5 us
    pallas_call x1, Pallas kernels, transform(): call(kernel, [shape], [pltpu.VMEM] * 7, [pltpu.VMEM], 'channel', scratch,...  7.52 us
    pallas_call x1, Pallas kernels, pack(): return packed(*inputs)[0]  3.66 us

profile of v1, /device:TPU:0, one launch (start us, length us, event | category | flops | bytes accessed | tf_op | source)
XLA Modules:
  0.0 71.9 jit_solution(14691965707676664179)
XLA Ops:
  0.6 3.7 %pack.1 = f32[128,24,128]{2,1,0:T(8,128)S(1)} custom-call(f32[1024,128]{1,0:T(8,128)} %signal_ref.1, f32[1024,128]{1,0:T(8,128)} %filter_ref.1, f32[1024,128]{1,0:T(8,128)} %grad_ref.1), custom_call_target="tpu_custom_call" | custom-call | tf_op jit(solution)/shard_map/pack/pallas_call | solution.py:231
  4.3 0.0 copy-start
  4.3 0.0 copy-start.1
  4.3 0.0 copy-start.2
  4.3 0.0 copy-start.3
  4.3 0.0 copy-start.4
  4.4 0.0 copy-start.5
  4.4 35.4 %all_to_all.10.refs_0_ = f32[128,24,128]{2,1,0:T(8,128)S(1)} all-to-all(f32[128,24,128]{2,1,0:T(8,128)S(1)} %pack.1), channel_id=1, replica_groups=mesh['gx'=16,'gy'=8] {'gx','gy'}, dimensions={0} | all-to-all | bytes 3145728 | tf_op jit(solution)/shard_map/all_to_all | solution.py:256
  39.7 0.0 copy-done
  39.7 0.0 copy-done.1
  39.7 0.0 copy-done.2
  39.8 0.0 copy-done.3
  39.8 0.0 copy-done.4
  39.8 0.0 copy-done.5
  39.8 7.5 %channel.1 = f32[128,16,128]{2,1,0:T(8,128)S(1)} custom-call(f32[128,24,128]{2,1,0:T(8,128)S(1)} %all_to_all.10.refs_0_, bf16[256,768]{1,0:T(8,128)(2,1)S(1)} %copy-done.2, bf16[256,768]{1,0:T(8,128)(2,1)S(1)} %copy-done.1, bf16[512,256]{1,0:T(8,128)(2,1)S(1)} %copy-done.4, bf16[512,256]{1,0:T(8,128)(2,1)S(1)} %copy-done.3, f32[8,2,128,128]{3,2,1,0:T(8,128)S(1)} %copy-done, ...), custom_call_target="tpu_custom_call" | custom-call | tf_op jit(solution)/shard_map/channel/pallas_call | solution.py:245
  47.3 23.1 %all_to_all.11.in_ref = f32[128,16,128]{2,1,0:T(8,128)S(1)} all-to-all(f32[128,16,128]{2,1,0:T(8,128)S(1)} %channel.1), channel_id=1, replica_groups=mesh['gx'=16,'gy'=8] {'gx','gy'}, dimensions={0} | all-to-all | bytes 2097152 | tf_op jit(solution)/shard_map/all_to_all | solution.py:256
  70.4 1.4 %unpack.1 = (f32[1024,128]{1,0:T(8,128)}, f32[1024,128]{1,0:T(8,128)}) custom-call(f32[128,16,128]{2,1,0:T(8,128)S(1)} %all_to_all.11.in_ref), custom_call_target="tpu_custom_call" | custom-call | tf_op jit(solution)/shard_map/unpack/pallas_call | solution.py:252
Async XLA Ops:
  4.3 35.5 %copy-start = (f32[8,2,128,128]{3,2,1,0:T(8,128)S(1)}, f32[8,2,128,128]{3,2,1,0:T(8,128)}, u32[]{:S(2)}) copy-start(f32[8,2,128,128]{3,2,1,0:T(8,128)} %constant.16.clone.refs_5_) | copy-start | bytes 3145732
  4.3 35.4 %copy-start.1 = (bf16[256,768]{1,0:T(8,128)(2,1)S(1)}, bf16[256,768]{1,0:T(8,128)(2,1)}, u32[]{:S(2)}) copy-start(bf16[256,768]{1,0:T(8,128)(2,1)} %constant.13.clone.refs_2_) | copy-start | bytes 1179652
  4.3 35.4 %copy-start.2 = (bf16[256,768]{1,0:T(8,128)(2,1)S(1)}, bf16[256,768]{1,0:T(8,128)(2,1)}, u32[]{:S(2)}) copy-start(bf16[256,768]{1,0:T(8,128)(2,1)} %constant.12.clone.refs_1_) | copy-start | bytes 1179652
  4.3 35.4 %copy-start.3 = (bf16[512,256]{1,0:T(8,128)(2,1)S(1)}, bf16[512,256]{1,0:T(8,128)(2,1)}, u32[]{:S(2)}) copy-start(bf16[512,256]{1,0:T(8,128)(2,1)} %constant.15.clone.refs_4_) | copy-start | bytes 786436
  4.3 35.4 %copy-start.4 = (bf16[512,256]{1,0:T(8,128)(2,1)S(1)}, bf16[512,256]{1,0:T(8,128)(2,1)}, u32[]{:S(2)}) copy-start(bf16[512,256]{1,0:T(8,128)(2,1)} %constant.14.clone.refs_3_) | copy-start | bytes 786436
  4.4 35.4 %copy-start.5 = (f32[2,128,128]{2,1,0:T(8,128)S(1)}, f32[2,128,128]{2,1,0:T(8,128)}, u32[]{:S(2)}) copy-start(f32[2,128,128]{2,1,0:T(8,128)} %constant.17.clone.refs_6_) | copy-start | bytes 393220

commit v2 on v1

--- a/solution.py
+++ b/solution.py
@@ -115,25 +115,21 @@
 
 
 def pack_kernel(signal_ref, filter_ref, grad_ref, out_ref, held, arrived):
-    refs = (signal_ref, filter_ref, grad_ref)
-    rows = signal_ref.shape[0] // B
     copies = []
-    for r in range(rows):
-        for q, ref in enumerate(refs):
-            here = pl.ds(r * B, B)
-            copies.append(pltpu.make_async_copy(ref.at[here], held.at[q, here], arrived.at[q, r]))
-            copies[-1].start()
-    for r in range(rows):
-        for q in range(3):
-            copies[3 * r + q].wait()
-            out_ref[:, 8 * q + r, :] = held[q, r * B : (r + 1) * B, :].T
+    for q, ref in enumerate((signal_ref, filter_ref, grad_ref)):
+        copies.append(pltpu.make_async_copy(ref, held.at[q], arrived.at[q]))
+        copies[-1].start()
+    for q, copy in enumerate(copies):
+        copy.wait()
+        for r in range(8):
+            out_ref[pl.ds(8 * q + r, B, stride=24), :] = held[q, r * B : (r + 1) * B, :].T
 
 
 def unpack_kernel(in_ref, first_ref, second_ref, held, left):
     copies = []
     for q, ref in enumerate((first_ref, second_ref)):
         for r in range(ref.shape[0] // B):
-            held[q, r * B : (r + 1) * B, :] = in_ref[:, 8 * q + r, :].T
+            held[q, r * B : (r + 1) * B, :] = in_ref[pl.ds(8 * q + r, B, stride=16), :].T
             here = pl.ds(r * B, B)
             copies.append(pltpu.make_async_copy(held.at[q, here], ref.at[here], left.at[q, r]))
             copies[-1].start()
@@ -142,69 +138,118 @@
 
 
 CHUNK = 16
+LAG = 2
+PAIRS = RADIX // 2
+CHUNKS = B // CHUNK
+
+
+def interleaved(tasks, fillers):
+    done, order = {}, []
+
+    def ready(needs, lag):
+        return all(need in done and len(order) - done[need] > lag for need in needs)
+
+    def emit(name, run):
+        run()
+        done[name] = len(order)
+        order.append(name)
+
+    tasks, fillers = list(tasks), list(fillers)
+    while tasks or fillers:
+        for lag in range(LAG, -1, -1):
+            found = next((task for task in tasks if ready(task[1], lag)), None)
+            if found:
+                break
+        if found:
+            tasks.remove(found)
+            emit(found[0], found[2])
+        filler = next((one for one in fillers if ready(one[1], 0)), None)
+        if filler:
+            fillers.remove(filler)
+            emit(filler[0], filler[2])
 
 
 def channel_kernel(scale, in_ref, left_ref, left_back_ref, right_ref, right_back_ref, inner_ref, outer_ref, out_ref, stage, back):
     blocks = in_ref.shape[0] // RADIX
-    for q in range(3):
-        for chunk in range(B // CHUNK):
-            rows = []
-            for a in range(RADIX):
-                start = a * blocks + chunk * (CHUNK // 8)
-                rows.append(in_ref[start : start + CHUNK // 8, 8 * q : 8 * q + 8, :].reshape(CHUNK, B))
-            here = slice(chunk * CHUNK, (chunk + 1) * CHUNK)
-            for m, pair in enumerate(spread(rows)):
-                real, imaginary = scaled(pair, (inner_ref[m, 0, here, :], -inner_ref[m, 1, here, :]))
-                lanes = slice((m % 2) * B, (m % 2 + 1) * B)
-                for part, value in enumerate((real, imaginary)):
-                    high, low = split(value)
-                    at = part * B + chunk * CHUNK
-                    stage[q, m // 2, at : at + CHUNK, lanes] = high
-                    stage[q, m // 2, 2 * B + at : 2 * B + at + CHUNK, lanes] = low
-    for pair_at in range(RADIX // 2):
-        spectra = []
-        for q in range(3):
-            mixed = left_product(left_ref, stage[q, pair_at])
-            turned = []
-            for half in range(2):
-                m = 2 * pair_at + half
-                lanes = slice(half * B, (half + 1) * B)
-                real, imaginary = scaled(
-                    (mixed[:B, lanes], mixed[B:, lanes]), (outer_ref[0], -outer_ref[1])
-                )
-                turned.append(jnp.concatenate([real, imaginary], axis=1))
-            high, low = split(jnp.concatenate(turned, axis=0))
-            spectra.append(right_product(high, low, right_ref))
-        grad_re, grad_im = spectra[2][:, :B], spectra[2][:, B:]
-        for q in range(2):
-            other_re, other_im = spectra[1 - q][:, :B], spectra[1 - q][:, B:]
-            product = jnp.concatenate(
-                [other_re * grad_re + other_im * grad_im, other_re * grad_im - other_im * grad_re], axis=1
-            )
-            high, low = split(product)
-            mixed = right_product(high, low, right_back_ref)
-            columns = []
-            for half in range(2):
-                m = 2 * pair_at + half
-                real, imaginary = scaled(
-                    (mixed[half * B : (half + 1) * B, :B], mixed[half * B : (half + 1) * B, B:]),
-                    (outer_ref[0], outer_ref[1]),
-                )
-                columns.append(jnp.concatenate([real, imaginary], axis=0))
-            high, low = split(jnp.concatenate(columns, axis=1))
-            back[q, pair_at] = left_product(left_back_ref, jnp.concatenate([high, low], axis=0))
-    for q in range(2):
-        for chunk in range(B // CHUNK):
-            here = slice(chunk * CHUNK, (chunk + 1) * CHUNK)
-            parts = []
-            for m in range(RADIX):
-                lanes = slice((m % 2) * B, (m % 2 + 1) * B)
-                at = chunk * CHUNK
-                pair = (back[q, m // 2, at : at + CHUNK, lanes], back[q, m // 2, B + at : B + at + CHUNK, lanes])
-                parts.append(scaled(pair, (inner_ref[m, 0, here, :], inner_ref[m, 1, here, :])))
-            for a, row in enumerate(gather_real(parts)):
-                start = a * blocks + chunk * (CHUNK // 8)
-                out_ref[start : start + CHUNK // 8, 8 * q : 8 * q + 8, :] = (row * scale).reshape(CHUNK // 8, 8, B)
+    mixed, spectra, returned = {}, {}, {}
+
+    def load(q, chunk):
+        rows = []
+        for a in range(RADIX):
+            start = a * blocks + chunk * (CHUNK // 8)
+            rows.append(in_ref[start : start + CHUNK // 8, 8 * q : 8 * q + 8, :].reshape(CHUNK, B))
+        here = slice(chunk * CHUNK, (chunk + 1) * CHUNK)
+        for m, pair in enumerate(spread(rows)):
+            parts = scaled(pair, (inner_ref[m, 0, here, :], -inner_ref[m, 1, here, :]))
+            lanes = slice((m % 2) * B, (m % 2 + 1) * B)
+            for part, value in enumerate(parts):
+                high, low = split(value)
+                at = part * B + chunk * CHUNK
+                stage[q, m // 2, at : at + CHUNK, lanes] = high
+                stage[q, m // 2, 2 * B + at : 2 * B + at + CHUNK, lanes] = low
+
+    def first(q, pair_at):
+        mixed[q, pair_at] = left_product(left_ref, stage[q, pair_at])
+
+    def second(q, pair_at):
+        value = mixed.pop((q, pair_at))
+        turned = []
+        for half in range(2):
+            lanes = slice(half * B, (half + 1) * B)
+            parts = scaled((value[:B, lanes], value[B:, lanes]), (outer_ref[0], -outer_ref[1]))
+            turned.append(jnp.concatenate(parts, axis=1))
+        high, low = split(jnp.concatenate(turned, axis=0))
+        spectra[q, pair_at] = right_product(high, low, right_ref)
+
+    def third(q, pair_at):
+        grad, other = spectra[2, pair_at], spectra[1 - q, pair_at]
+        grad_re, grad_im, other_re, other_im = grad[:, :B], grad[:, B:], other[:, :B], other[:, B:]
+        real = other_re * grad_re + other_im * grad_im
+        imaginary = other_re * grad_im - other_im * grad_re
+        high, low = split(jnp.concatenate([real, imaginary], axis=1))
+        returned[q, pair_at] = right_product(high, low, right_back_ref)
+
+    def fourth(q, pair_at):
+        value = returned.pop((q, pair_at))
+        columns = []
+        for half in range(2):
+            rows = slice(half * B, (half + 1) * B)
+            parts = scaled((value[rows, :B], value[rows, B:]), (outer_ref[0], outer_ref[1]))
+            columns.append(jnp.concatenate(parts, axis=0))
+        high, low = split(jnp.concatenate(columns, axis=1))
+        back[q, pair_at] = left_product(left_back_ref, jnp.concatenate([high, low], axis=0))
+
+    def store(q, chunk):
+        at = chunk * CHUNK
+        parts = []
+        for m in range(RADIX):
+            lanes = slice((m % 2) * B, (m % 2 + 1) * B)
+            pair = (back[q, m // 2, at : at + CHUNK, lanes], back[q, m // 2, B + at : B + at + CHUNK, lanes])
+            table = (inner_ref[m, 0, at : at + CHUNK, :], inner_ref[m, 1, at : at + CHUNK, :])
+            parts.append(scaled(pair, table))
+        for a, row in enumerate(gather_real(parts)):
+            start = a * blocks + chunk * (CHUNK // 8)
+            out_ref[start : start + CHUNK // 8, 8 * q : 8 * q + 8, :] = (row * scale).reshape(CHUNK // 8, 8, B)
+
+    def task(run, q, at, needs):
+        return (run.__name__, q, at), needs, lambda: run(q, at)
+
+    tasks, fillers = [], []
+    for q in (2, 0, 1):
+        loads = [("load", q, chunk) for chunk in range(CHUNKS)]
+        fillers += [task(load, q, chunk, []) for chunk in range(CHUNKS)]
+        for pair_at in range(PAIRS):
+            tasks.append(task(second, q, pair_at, [("first", q, pair_at)]))
+            tasks.append(task(first, q, pair_at, loads))
+        if q != 2:
+            for pair_at in range(PAIRS):
+                out = 1 - q
+                tasks.append(task(fourth, out, pair_at, [("third", out, pair_at)]))
+                needs = [("second", 2, pair_at), ("second", q, pair_at)]
+                tasks.append(task(third, out, pair_at, needs))
+            needs = [("fourth", out, pair_at) for pair_at in range(PAIRS)]
+            fillers += [task(store, out, chunk, needs) for chunk in range(CHUNKS)]
+    interleaved(tasks, fillers)
 
 
 def call(kernel, out_shape, in_spaces, out_spaces, name, scratch, interpret):
@@ -222,13 +267,13 @@
 
 def pack(signal, filter_taps, grad_out, interpret=False):
     rows = signal.shape[0]
-    shape = jax.ShapeDtypeStruct((B, 24, B), f32)
-    scratch = [pltpu.VMEM((3, rows, B), f32), pltpu.SemaphoreType.DMA((3, rows // B))]
+    shape = jax.ShapeDtypeStruct((24 * B, B), f32)
+    scratch = [pltpu.VMEM((3, rows, B), f32), pltpu.SemaphoreType.DMA((3,))]
     packed = call(pack_kernel, [shape], [pltpu.HBM] * 3, [pltpu.VMEM], "pack", scratch, interpret)
     inputs = (signal, filter_taps, grad_out)
     if not interpret:
         inputs = [pltpu.with_memory_space_constraint(x, pltpu.HBM) for x in inputs]
-    return packed(*inputs)[0]
+    return packed(*inputs)[0].reshape(B, 24, B)
 
 
 def transform(received, interpret=False):
@@ -249,7 +294,7 @@
     rows = 8 * B
     shape = jax.ShapeDtypeStruct((rows, B), f32)
     scratch = [pltpu.VMEM((2, rows, B), f32), pltpu.SemaphoreType.DMA((2, rows // B))]
-    return call(unpack_kernel, [shape] * 2, [pltpu.VMEM], [pltpu.HBM] * 2, "unpack", scratch, interpret)(received)
+    return call(unpack_kernel, [shape] * 2, [pltpu.VMEM], [pltpu.HBM] * 2, "unpack", scratch, interpret)(received.reshape(16 * B, B))
 
 
 def exchange(array):

time: 72.1 us -> 69.2 us (0.960)
  Pallas kernels: 12.6 us -> 9.77 us
    pallas_call x1, Pallas kernels: 3.66 us -> 1.68 us  [pack(): return packed(*inputs)[0].reshape(B, 24, B)]
where the time goes in v2:
time: 69.2 us; the launch traced here: 69 us
  blocking collectives  58.5 us (85%)
  Pallas kernels  9.77 us (14%)
  between operations  0.72 us (1%)
    all_to_all x2, blocking collectives, exchange(): return lax.all_to_all(array, AXES, split_axis=0, concat_axis=0, tiled=True)  58.5 us
    pallas_call x1, Pallas kernels, transform(): call(kernel, [shape], [pltpu.VMEM] * 7, [pltpu.VMEM], 'channel', scratch,...  6.9 us
    pallas_call x1, Pallas kernels, pack(): return packed(*inputs)[0].reshape(B, 24, B)  1.68 us

profile of v2, /device:TPU:0, one launch (start us, length us, event | category | flops | bytes accessed | tf_op | source)
XLA Modules:
  0.0 69.0 jit_solution(1254720569105395282)
XLA Ops:
  0.6 1.7 %pack.1 = f32[3072,128]{1,0:T(8,128)S(1)} custom-call(f32[1024,128]{1,0:T(8,128)} %signal_ref.1, f32[1024,128]{1,0:T(8,128)} %filter_ref.1, f32[1024,128]{1,0:T(8,128)} %grad_ref.1), custom_call_target="tpu_custom_call" | custom-call | tf_op jit(solution)/shard_map/pack/pallas_call | solution.py:276
  2.3 0.0 copy-start
  2.3 0.0 copy-start.1
  2.3 0.0 copy-start.2
  2.4 0.0 copy-start.3
  2.4 0.0 copy-start.4
  2.4 0.0 copy-start.5
  2.4 35.4 %all_to_all.10.refs_0_ = f32[128,24,128]{2,1,0:T(8,128)S(1)} all-to-all(f32[128,24,128]{2,1,0:T(8,128)S(1)} %bitcast.2), channel_id=1, replica_groups=mesh['gx'=16,'gy'=8] {'gx','gy'}, dimensions={0} | all-to-all | bytes 3145728 | tf_op jit(solution)/shard_map/all_to_all | solution.py:301
  37.8 0.0 copy-done
  37.8 0.0 copy-done.1
  37.8 0.0 copy-done.2
  37.8 0.0 copy-done.3
  37.8 0.0 copy-done.4
  37.8 0.0 copy-done.5
  37.8 6.9 %channel.1 = f32[128,16,128]{2,1,0:T(8,128)S(1)} custom-call(f32[128,24,128]{2,1,0:T(8,128)S(1)} %all_to_all.10.refs_0_, bf16[256,768]{1,0:T(8,128)(2,1)S(1)} %copy-done.2, bf16[256,768]{1,0:T(8,128)(2,1)S(1)} %copy-done.1, bf16[512,256]{1,0:T(8,128)(2,1)S(1)} %copy-done.4, bf16[512,256]{1,0:T(8,128)(2,1)S(1)} %copy-done.3, f32[8,2,128,128]{3,2,1,0:T(8,128)S(1)} %copy-done, ...), custom_call_target="tpu_custom_call" | custom-call | tf_op jit(solution)/shard_map/channel/pallas_call | solution.py:290
  44.7 23.1 %all_to_all.11 = f32[128,16,128]{2,1,0:T(8,128)S(1)} all-to-all(f32[128,16,128]{2,1,0:T(8,128)S(1)} %channel.1), channel_id=1, replica_groups=mesh['gx'=16,'gy'=8] {'gx','gy'}, dimensions={0} | all-to-all | bytes 2097152 | tf_op jit(solution)/shard_map/all_to_all | solution.py:301
  67.8 1.2 %unpack.1 = (f32[1024,128]{1,0:T(8,128)}, f32[1024,128]{1,0:T(8,128)}) custom-call(f32[2048,128]{1,0:T(8,128)S(1)} %bitcast.3), custom_call_target="tpu_custom_call" | custom-call | tf_op jit(solution)/shard_map/unpack/pallas_call | solution.py:297
Async XLA Ops:
  2.3 35.5 %copy-start = (f32[8,2,128,128]{3,2,1,0:T(8,128)S(1)}, f32[8,2,128,128]{3,2,1,0:T(8,128)}, u32[]{:S(2)}) copy-start(f32[8,2,128,128]{3,2,1,0:T(8,128)} %constant.16.clone.refs_5_) | copy-start | bytes 3145732
  2.3 35.4 %copy-start.1 = (bf16[256,768]{1,0:T(8,128)(2,1)S(1)}, bf16[256,768]{1,0:T(8,128)(2,1)}, u32[]{:S(2)}) copy-start(bf16[256,768]{1,0:T(8,128)(2,1)} %constant.13.clone.refs_2_) | copy-start | bytes 1179652
  2.3 35.4 %copy-start.2 = (bf16[256,768]{1,0:T(8,128)(2,1)S(1)}, bf16[256,768]{1,0:T(8,128)(2,1)}, u32[]{:S(2)}) copy-start(bf16[256,768]{1,0:T(8,128)(2,1)} %constant.12.clone.refs_1_) | copy-start | bytes 1179652
  2.4 35.4 %copy-start.3 = (bf16[512,256]{1,0:T(8,128)(2,1)S(1)}, bf16[512,256]{1,0:T(8,128)(2,1)}, u32[]{:S(2)}) copy-start(bf16[512,256]{1,0:T(8,128)(2,1)} %constant.15.clone.refs_4_) | copy-start | bytes 786436
  2.4 35.4 %copy-start.4 = (bf16[512,256]{1,0:T(8,128)(2,1)S(1)}, bf16[512,256]{1,0:T(8,128)(2,1)}, u32[]{:S(2)}) copy-start(bf16[512,256]{1,0:T(8,128)(2,1)} %constant.14.clone.refs_3_) | copy-start | bytes 786436
  2.4 35.4 %copy-start.5 = (f32[2,128,128]{2,1,0:T(8,128)S(1)}, f32[2,128,128]{2,1,0:T(8,128)}, u32[]{:S(2)}) copy-start(f32[2,128,128]{2,1,0:T(8,128)} %constant.17.clone.refs_6_) | copy-start | bytes 393220

commit v3 on v2

--- a/solution.py
+++ b/solution.py
@@ -29,10 +29,11 @@
     cosine, sine = turn((index[:, None] * index[None, :] % B) / B)
     left = np.block([[cosine, sine], [-sine, cosine]])
     left_back = np.block([[cosine, -sine], [sine, cosine]])
+    scale = 1.0 / length
     packed = []
-    for matrix in (left, left_back):
+    for matrix in (left, left_back * scale):
         high, low = halves(matrix)
-        packed.append(np.concatenate([high, high, low], axis=1))
+        packed.append(np.concatenate([high, low], axis=1))
     for matrix in (left.T, left_back.T):
         high, low = halves(matrix)
         packed.append(np.concatenate([high, low], axis=0))
@@ -49,48 +50,47 @@
     return real * cosine - imaginary * sine, real * sine + imaginary * cosine
 
 
+def butterfly(points, sign):
+    (r0, i0), (r1, i1), (r2, i2), (r3, i3) = points
+    er, ei, fr, fi = r0 + r2, i0 + i2, r0 - r2, i0 - i2
+    gr, gi, hr, hi = r1 + r3, i1 + i3, r1 - r3, i1 - i3
+    middle = [(fr + hi, fi - hr), (fr - hi, fi + hr)]
+    return (er + gr, ei + gi), middle[sign > 0], (er - gr, ei - gi), middle[sign < 0]
+
+
+def constants_of(a, odd):
+    near, far = turn(a * (odd + 0.25) / RADIX), turn((a + 4) * (odd + 0.25) / RADIX)
+    return [np.float32(value) for value in (*near, *far)]
+
+
 def spread(rows):
     root = np.float32(np.sqrt(0.5))
     out = [None] * RADIX
-    halfway = [rows[a + 4] * root for a in range(4)]
+    far = rows[4] * root
     for odd in range(2):
-        points = []
-        for a in range(4):
-            if odd:
-                pair = (rows[a] - halfway[a], halfway[a])
-            else:
-                pair = (rows[a] + halfway[a], -halfway[a])
-            if a:
-                cosine, sine = turn(-a * (odd + 0.25) / RADIX)
-                pair = scaled(pair, (np.float32(cosine), np.float32(sine)))
-            points.append(pair)
-        (r0, i0), (r1, i1), (r2, i2), (r3, i3) = points
-        er, ei, fr, fi = r0 + r2, i0 + i2, r0 - r2, i0 - i2
-        gr, gi, hr, hi = r1 + r3, i1 + i3, r1 - r3, i1 - i3
-        out[odd] = (er + gr, ei + gi)
-        out[2 + odd] = (fr + hi, fi - hr)
-        out[4 + odd] = (er - gr, ei - gi)
-        out[6 + odd] = (fr - hi, fi + hr)
+        points = [(rows[0] - far, far) if odd else (rows[0] + far, -far)]
+        for a in range(1, 4):
+            cosine, sine, far_cosine, far_sine = constants_of(a, odd)
+            real = rows[a] * cosine + rows[a + 4] * far_cosine
+            points.append((real, rows[a] * -sine + rows[a + 4] * -far_sine))
+        for n, pair in enumerate(butterfly(points, -1)):
+            out[2 * n + odd] = pair
     return out
 
 
 def gather_real(parts):
     root = np.float32(np.sqrt(0.5))
+    even, odd = (butterfly([parts[2 * n + one] for n in range(4)], 1) for one in range(2))
     rows = [None] * RADIX
-    both = []
-    for odd in range(2):
-        (r0, i0), (r1, i1), (r2, i2), (r3, i3) = (parts[2 * n + odd] for n in range(4))
-        er, ei, fr, fi = r0 + r2, i0 + i2, r0 - r2, i0 - i2
-        gr, gi, hr, hi = r1 + r3, i1 + i3, r1 - r3, i1 - i3
-        points = [(er + gr, ei + gi), (fr - hi, fi + hr), (er - gr, ei - gi), (fr + hi, fi - hr)]
-        for a in range(1, 4):
-            cosine, sine = turn(a * (odd + 0.25) / RADIX)
-            points[a] = scaled(points[a], (np.float32(cosine), np.float32(sine)))
-        both.append(points)
-    for a in range(4):
-        (er, ei), (fr, fi) = both[0][a], both[1][a]
-        rows[a] = er + fr
-        rows[a + 4] = ((er - fr) - (ei - fi)) * root
+    rows[0] = even[0][0] + odd[0][0]
+    rows[4] = ((even[0][0] - odd[0][0]) - (even[0][1] - odd[0][1])) * root
+    for a in range(1, 4):
+        first, second = constants_of(a, 0), constants_of(a, 1)
+        for far in range(2):
+            cosine, sine = first[2 * far : 2 * far + 2]
+            other_cosine, other_sine = second[2 * far : 2 * far + 2]
+            total = even[a][0] * cosine - even[a][1] * sine
+            rows[a + 4 * far] = total + (odd[a][0] * other_cosine - odd[a][1] * other_sine)
     return rows
 
 
@@ -100,8 +100,12 @@
 
 
 def left_product(matrix_ref, data):
-    return jnp.dot(matrix_ref[:, : 4 * B], data, preferred_element_type=f32) + jnp.dot(
-        matrix_ref[:, 4 * B :], data[: 2 * B], preferred_element_type=f32
+    high, low = data[: 2 * B], data[2 * B :]
+    top = matrix_ref[:, : 2 * B]
+    return (
+        jnp.dot(top, high, preferred_element_type=f32)
+        + jnp.dot(matrix_ref[:, 2 * B :], high, preferred_element_type=f32)
+        + jnp.dot(top, low, preferred_element_type=f32)
     )
 
 
@@ -109,8 +113,8 @@
     top = matrix_ref[: 2 * B, :]
     return (
         jnp.dot(high, top, preferred_element_type=f32)
+        + jnp.dot(high, matrix_ref[2 * B :, :], preferred_element_type=f32)
         + jnp.dot(low, top, preferred_element_type=f32)
-        + jnp.dot(high, matrix_ref[2 * B :, :], preferred_element_type=f32)
     )
 
 
@@ -138,38 +142,23 @@
 
 
 CHUNK = 16
-LAG = 2
-PAIRS = RADIX // 2
+WIDE = 2
+PAIRS = RADIX // WIDE
 CHUNKS = B // CHUNK
 
 
 def interleaved(tasks, fillers):
-    done, order = {}, []
-
-    def ready(needs, lag):
-        return all(need in done and len(order) - done[need] > lag for need in needs)
-
-    def emit(name, run):
-        run()
-        done[name] = len(order)
-        order.append(name)
-
-    tasks, fillers = list(tasks), list(fillers)
+    done = set()
     while tasks or fillers:
-        for lag in range(LAG, -1, -1):
-            found = next((task for task in tasks if ready(task[1], lag)), None)
+        for names in (tasks, fillers):
+            found = next((one for one in names if done.issuperset(one[1])), None)
             if found:
-                break
-        if found:
-            tasks.remove(found)
-            emit(found[0], found[2])
-        filler = next((one for one in fillers if ready(one[1], 0)), None)
-        if filler:
-            fillers.remove(filler)
-            emit(filler[0], filler[2])
-
-
-def channel_kernel(scale, in_ref, left_ref, left_back_ref, right_ref, right_back_ref, inner_ref, outer_ref, out_ref, stage, back):
+                names.remove(found)
+                found[2]()
+                done.add(found[0])
+
+
+def channel_kernel(in_ref, left_ref, left_back_ref, right_ref, right_back_ref, inner_ref, outer_ref, out_ref, stage, back):
     blocks = in_ref.shape[0] // RADIX
     mixed, spectra, returned = {}, {}, {}
 
@@ -181,12 +170,12 @@
         here = slice(chunk * CHUNK, (chunk + 1) * CHUNK)
         for m, pair in enumerate(spread(rows)):
             parts = scaled(pair, (inner_ref[m, 0, here, :], -inner_ref[m, 1, here, :]))
-            lanes = slice((m % 2) * B, (m % 2 + 1) * B)
+            lanes = slice(m % WIDE * B, (m % WIDE + 1) * B)
             for part, value in enumerate(parts):
                 high, low = split(value)
                 at = part * B + chunk * CHUNK
-                stage[q, m // 2, at : at + CHUNK, lanes] = high
-                stage[q, m // 2, 2 * B + at : 2 * B + at + CHUNK, lanes] = low
+                stage[q, m // WIDE, at : at + CHUNK, lanes] = high
+                stage[q, m // WIDE, 2 * B + at : 2 * B + at + CHUNK, lanes] = low
 
     def first(q, pair_at):
         mixed[q, pair_at] = left_product(left_ref, stage[q, pair_at])
@@ -194,7 +183,7 @@
     def second(q, pair_at):
         value = mixed.pop((q, pair_at))
         turned = []
-        for half in range(2):
+        for half in range(WIDE):
             lanes = slice(half * B, (half + 1) * B)
             parts = scaled((value[:B, lanes], value[B:, lanes]), (outer_ref[0], -outer_ref[1]))
             turned.append(jnp.concatenate(parts, axis=1))
@@ -212,7 +201,7 @@
     def fourth(q, pair_at):
         value = returned.pop((q, pair_at))
         columns = []
-        for half in range(2):
+        for half in range(WIDE):
             rows = slice(half * B, (half + 1) * B)
             parts = scaled((value[rows, :B], value[rows, B:]), (outer_ref[0], outer_ref[1]))
             columns.append(jnp.concatenate(parts, axis=0))
@@ -223,13 +212,13 @@
         at = chunk * CHUNK
         parts = []
         for m in range(RADIX):
-            lanes = slice((m % 2) * B, (m % 2 + 1) * B)
-            pair = (back[q, m // 2, at : at + CHUNK, lanes], back[q, m // 2, B + at : B + at + CHUNK, lanes])
+            lanes = slice(m % WIDE * B, (m % WIDE + 1) * B)
+            pair = (back[q, m // WIDE, at : at + CHUNK, lanes], back[q, m // WIDE, B + at : B + at + CHUNK, lanes])
             table = (inner_ref[m, 0, at : at + CHUNK, :], inner_ref[m, 1, at : at + CHUNK, :])
             parts.append(scaled(pair, table))
         for a, row in enumerate(gather_real(parts)):
             start = a * blocks + chunk * (CHUNK // 8)
-            out_ref[start : start + CHUNK // 8, 8 * q : 8 * q + 8, :] = (row * scale).reshape(CHUNK // 8, 8, B)
+            out_ref[start : start + CHUNK // 8, 8 * q : 8 * q + 8, :] = row.reshape(CHUNK // 8, 8, B)
 
     def task(run, q, at, needs):
         return (run.__name__, q, at), needs, lambda: run(q, at)
@@ -282,12 +271,9 @@
     packed, inner, outer = tables(length)
     constants = [jnp.asarray(table) for table in packed] + [jnp.asarray(inner), jnp.asarray(outer)]
 
-    def kernel(*refs):
-        channel_kernel(np.float32(1.0 / length), *refs)
-
     shape = jax.ShapeDtypeStruct((blocks, 16, B), f32)
-    scratch = [pltpu.VMEM((3, RADIX // 2, 4 * B, 2 * B), bf16), pltpu.VMEM((2, RADIX // 2, 2 * B, 2 * B), f32)]
-    return call(kernel, [shape], [pltpu.VMEM] * 7, [pltpu.VMEM], "channel", scratch, interpret)(received, *constants)[0]
+    scratch = [pltpu.VMEM((3, PAIRS, 4 * B, WIDE * B), bf16), pltpu.VMEM((2, PAIRS, 2 * B, WIDE * B), f32)]
+    return call(channel_kernel, [shape], [pltpu.VMEM] * 7, [pltpu.VMEM], "channel", scratch, interpret)(received, *constants)[0]
 
 
 def unpack(received, interpret=False):

time: 69.2 us -> 68.2 us (0.986)
  Pallas kernels: 9.77 us -> 8.81 us
    pallas_call x1, Pallas kernels: 6.9 us -> 5.94 us  [transform(): call(channel_kernel, [shape], [pltpu.VMEM] * 7, [pltpu.VMEM], 'channel',...]
where the time goes in v3:
time: 68.2 us; the launch traced here: 68.1 us
  blocking collectives  58.5 us (86%)
  Pallas kernels  8.81 us (13%)
  between operations  0.72 us (1%)
    all_to_all x2, blocking collectives, exchange(): return lax.all_to_all(array, AXES, split_axis=0, concat_axis=0, tiled=True)  58.5 us
    pallas_call x1, Pallas kernels, transform(): call(channel_kernel, [shape], [pltpu.VMEM] * 7, [pltpu.VMEM], 'channel',...  5.94 us
    pallas_call x1, Pallas kernels, pack(): return packed(*inputs)[0].reshape(B, 24, B)  1.68 us

profile of v3, /device:TPU:0, one launch (start us, length us, event | category | flops | bytes accessed | tf_op | source)
XLA Modules:
  0.0 68.1 jit_solution(4963255322501918474)
XLA Ops:
  0.6 1.7 %pack.1 = f32[3072,128]{1,0:T(8,128)S(1)} custom-call(f32[1024,128]{1,0:T(8,128)} %signal_ref.1, f32[1024,128]{1,0:T(8,128)} %filter_ref.1, f32[1024,128]{1,0:T(8,128)} %grad_ref.1), custom_call_target="tpu_custom_call" | custom-call | tf_op jit(solution)/shard_map/pack/pallas_call | solution.py:265
  2.3 0.0 copy-start
  2.3 0.0 copy-start.1
  2.3 0.0 copy-start.2
  2.4 0.0 copy-start.3
  2.4 0.0 copy-start.4
  2.4 0.0 copy-start.5
  2.4 35.4 %all_to_all.10.in_ref = f32[128,24,128]{2,1,0:T(8,128)S(1)} all-to-all(f32[128,24,128]{2,1,0:T(8,128)S(1)} %bitcast.2), channel_id=1, replica_groups=mesh['gx'=16,'gy'=8] {'gx','gy'}, dimensions={0} | all-to-all | bytes 3145728 | tf_op jit(solution)/shard_map/all_to_all | solution.py:287
  37.8 0.0 copy-done
  37.8 0.0 copy-done.1
  37.8 0.0 copy-done.2
  37.8 0.0 copy-done.3
  37.8 0.0 copy-done.4
  37.8 0.0 copy-done.5
  37.8 5.9 %channel.1 = f32[128,16,128]{2,1,0:T(8,128)S(1)} custom-call(f32[128,24,128]{2,1,0:T(8,128)S(1)} %all_to_all.10.in_ref, bf16[256,512]{1,0:T(8,128)(2,1)S(1)} %copy-done.4, bf16[256,512]{1,0:T(8,128)(2,1)S(1)} %copy-done.3, bf16[512,256]{1,0:T(8,128)(2,1)S(1)} %copy-done.2, bf16[512,256]{1,0:T(8,128)(2,1)S(1)} %copy-done.1, f32[8,2,128,128]{3,2,1,0:T(8,128)S(1)} %copy-done, ...), custom_call_target="tpu_custom_call" | custom-call | tf_op jit(solution)/shard_map/channel/pallas_call | solution.py:276
  43.8 23.1 %all_to_all.11 = f32[128,16,128]{2,1,0:T(8,128)S(1)} all-to-all(f32[128,16,128]{2,1,0:T(8,128)S(1)} %channel.1), channel_id=1, replica_groups=mesh['gx'=16,'gy'=8] {'gx','gy'}, dimensions={0} | all-to-all | bytes 2097152 | tf_op jit(solution)/shard_map/all_to_all | solution.py:287
  66.9 1.2 %unpack.1 = (f32[1024,128]{1,0:T(8,128)}, f32[1024,128]{1,0:T(8,128)}) custom-call(f32[2048,128]{1,0:T(8,128)S(1)} %bitcast.3), custom_call_target="tpu_custom_call" | custom-call | tf_op jit(solution)/shard_map/unpack/pallas_call | solution.py:283
Async XLA Ops:
  2.3 35.5 %copy-start = (f32[8,2,128,128]{3,2,1,0:T(8,128)S(1)}, f32[8,2,128,128]{3,2,1,0:T(8,128)}, u32[]{:S(2)}) copy-start(f32[8,2,128,128]{3,2,1,0:T(8,128)} %constant.16.clone.inner_ref) | copy-start | bytes 3145732
  2.3 35.4 %copy-start.1 = (bf16[512,256]{1,0:T(8,128)(2,1)S(1)}, bf16[512,256]{1,0:T(8,128)(2,1)}, u32[]{:S(2)}) copy-start(bf16[512,256]{1,0:T(8,128)(2,1)} %constant.15.clone.right_back_ref) | copy-start | bytes 786436
  2.3 35.4 %copy-start.2 = (bf16[512,256]{1,0:T(8,128)(2,1)S(1)}, bf16[512,256]{1,0:T(8,128)(2,1)}, u32[]{:S(2)}) copy-start(bf16[512,256]{1,0:T(8,128)(2,1)} %constant.14.clone.right_ref) | copy-start | bytes 786436
  2.4 35.4 %copy-start.3 = (bf16[256,512]{1,0:T(8,128)(2,1)S(1)}, bf16[256,512]{1,0:T(8,128)(2,1)}, u32[]{:S(2)}) copy-start(bf16[256,512]{1,0:T(8,128)(2,1)} %constant.13.clone.left_back_ref) | copy-start | bytes 786436
  2.4 35.4 %copy-start.4 = (bf16[256,512]{1,0:T(8,128)(2,1)S(1)}, bf16[256,512]{1,0:T(8,128)(2,1)}, u32[]{:S(2)}) copy-start(bf16[256,512]{1,0:T(8,128)(2,1)} %constant.12.clone.left_ref) | copy-start | bytes 786436
  2.4 35.4 %copy-start.5 = (f32[2,128,128]{2,1,0:T(8,128)S(1)}, f32[2,128,128]{2,1,0:T(8,128)}, u32[]{:S(2)}) copy-start(f32[2,128,128]{2,1,0:T(8,128)} %constant.17.clone.outer_ref) | copy-start | bytes 393220

commit v4 on v3

v4 whole, which is shorter than its diff:
```python
import jax
import jax.numpy as jnp
import numpy as np
from jax import lax
from jax.experimental import pallas as pl
from jax.experimental.pallas import tpu as pltpu
from jax.sharding import PartitionSpec as P

f32 = jnp.float32
bf16 = jnp.bfloat16
AXES = ("gx", "gy")
B = 128
RADIX = 8


def turn(count):
    angle = 2.0 * np.pi * count
    return np.cos(angle), np.sin(angle)


def halves(matrix):
    high = matrix.astype(np.float32).astype(jnp.bfloat16)
    low = (matrix - high.astype(np.float64)).astype(np.float32).astype(jnp.bfloat16)
    return high, low


def tables(length):
    index = np.arange(B)
    cosine, sine = turn(index[None, :] * (4 * index[:, None] + 1) % (4 * B) / (4 * B))
    high, low = halves(np.concatenate([cosine, -sine], axis=0))
    packed = [np.concatenate([high, high, low], axis=1)]
    high, low = halves(np.concatenate([cosine.T, -sine.T], axis=1) / length)
    packed.append(np.concatenate([high, low], axis=1))
    cosine, sine = turn((index[:, None] * index[None, :] % B) / B)
    for matrix in (np.block([[cosine, -sine], [sine, cosine]]), np.block([[cosine, sine], [-sine, cosine]])):
        high, low = halves(matrix)
        packed.append(np.concatenate([high, low], axis=0))
    r = np.arange(RADIX)
    position = B * r[:, None, None] + index[None, None, :]
    inner = np.stack(turn(position * (4 * index[None, :, None] + 1) % (4 * length) / (4 * length)), axis=1)
    outer = np.concatenate(turn(r[:, None] * index[None, :] / (RADIX * B)))
    return packed, inner.astype(np.float32), outer.astype(np.float32)


def scaled(pair, constant):
    real, imaginary = pair
    cosine, sine = constant
    return real * cosine - imaginary * sine, real * sine + imaginary * cosine


def butterfly(points, sign):
    (r0, i0), (r1, i1), (r2, i2), (r3, i3) = points
    er, ei, fr, fi = r0 + r2, i0 + i2, r0 - r2, i0 - i2
    gr, gi, hr, hi = r1 + r3, i1 + i3, r1 - r3, i1 - i3
    middle = [(fr + hi, fi - hr), (fr - hi, fi + hr)]
    return (er + gr, ei + gi), middle[sign > 0], (er - gr, ei - gi), middle[sign < 0]


def eighths(points, sign):
    root = np.float32(np.sqrt(0.5))
    even, odd = butterfly(points[0::2], sign), butterfly(points[1::2], sign)
    (r1, i1), (r2, i2), (r3, i3) = odd[1:]
    if sign < 0:
        turned = [odd[0], ((r1 + i1) * root, (i1 - r1) * root), (i2, -r2), ((i3 - r3) * root, -(i3 + r3) * root)]
    else:
        turned = [odd[0], ((r1 - i1) * root, (i1 + r1) * root), (-i2, r2), (-(r3 + i3) * root, (r3 - i3) * root)]
    plus = [(e[0] + o[0], e[1] + o[1]) for e, o in zip(even, turned)]
    return plus + [(e[0] - o[0], e[1] - o[1]) for e, o in zip(even, turned)]


def split(value):
    high = value.astype(bf16)
    return high, (value - high.astype(f32)).astype(bf16)


def right_product(high, low, matrix_ref):
    top = matrix_ref[: 2 * B, :]
    return (
        jnp.dot(high, top, preferred_element_type=f32)
        + jnp.dot(high, matrix_ref[2 * B :, :], preferred_element_type=f32)
        + jnp.dot(low, top, preferred_element_type=f32)
    )


def pack_kernel(signal_ref, filter_ref, grad_ref, out_ref, held, arrived):
    copies = []
    for q, ref in enumerate((signal_ref, filter_ref, grad_ref)):
        copies.append(pltpu.make_async_copy(ref, held.at[q], arrived.at[q]))
        copies[-1].start()
    for q, copy in enumerate(copies):
        copy.wait()
        for r in range(8):
            out_ref[pl.ds(8 * q + r, B, stride=24), :] = held[q, r * B : (r + 1) * B, :].T


def unpack_kernel(in_ref, first_ref, second_ref, held, left):
    copies = []
    for q, ref in enumerate((first_ref, second_ref)):
        for r in range(ref.shape[0] // B):
            held[q, r * B : (r + 1) * B, :] = in_ref[pl.ds(8 * q + r, B, stride=16), :].T
            here = pl.ds(r * B, B)
            copies.append(pltpu.make_async_copy(held.at[q, here], ref.at[here], left.at[q, r]))
            copies[-1].start()
    for copy in copies:
        copy.wait()


CHUNK = 16
PAIRS = RADIX // 2
CHUNKS = B // CHUNK


def interleaved(tasks, fillers):
    done = set()
    while tasks or fillers:
        for names in (tasks, fillers, fillers):
            found = next((one for one in names if done.issuperset(one[1])), None)
            if found:
                names.remove(found)
                found[2]()
                done.add(found[0])


def channel_kernel(
    in_ref, left_ref, left_back_ref, right_ref, right_back_ref, inner_ref, outer_ref, out_ref,
    start, mixed, high_ref, low_ref, returned, last,
):
    spectra = {}

    def lanes_of(n):
        return slice(n % 2 * B, (n % 2 + 1) * B)

    def outer(m, sign):
        return outer_ref[m : m + 1, :], sign * outer_ref[RADIX + m : RADIX + m + 1, :]

    def enter(q, d):
        high, low = split(in_ref[pl.ds(8 * q + d, B, stride=24), :])
        start[q, d // 2, :B, lanes_of(d)] = high
        start[q, d // 2, B:, lanes_of(d)] = low

    def first(q, pair_at):
        data = start[q, pair_at]
        mixed[q, pair_at] = jnp.dot(left_ref[:, : 2 * B], data, preferred_element_type=f32) + jnp.dot(
            left_ref[:, 2 * B :], data[:B], preferred_element_type=f32
        )

    def middle(q, chunk):
        here = slice(chunk * CHUNK, (chunk + 1) * CHUNK)
        under = slice(B + chunk * CHUNK, B + (chunk + 1) * CHUNK)
        points = []
        for d in range(RADIX):
            pair = mixed[q, d // 2, here, lanes_of(d)], mixed[q, d // 2, under, lanes_of(d)]
            points.append(scaled(pair, (inner_ref[d, 0, here, :], -inner_ref[d, 1, here, :])))
        for m, pair in enumerate(eighths(points, -1)):
            if m:
                pair = scaled(pair, outer(m, -1))
            for part, value in enumerate(pair):
                high, low = split(value)
                rows, lanes = slice(m * B + chunk * CHUNK, m * B + (chunk + 1) * CHUNK), lanes_of(part)
                high_ref[q, rows, lanes] = high
                low_ref[q, rows, lanes] = low

    def second(q, pair_at):
        rows = slice(pair_at * 2 * B, (pair_at + 1) * 2 * B)
        spectra[q, pair_at] = right_product(high_ref[q, rows, :], low_ref[q, rows, :], right_ref)

    def third(q, pair_at):
        grad, other = spectra[2, pair_at], spectra[1 - q, pair_at]
        grad_re, grad_im, other_re, other_im = grad[:, :B], grad[:, B:], other[:, :B], other[:, B:]
        real = other_re * grad_re + other_im * grad_im
        imaginary = other_re * grad_im - other_im * grad_re
        high, low = split(jnp.concatenate([real, imaginary], axis=1))
        returned[q, pair_at] = right_product(high, low, right_back_ref)

    def middle_back(q, chunk):
        here = slice(chunk * CHUNK, (chunk + 1) * CHUNK)
        points = []
        for m in range(RADIX):
            rows = slice(m % 2 * B + chunk * CHUNK, m % 2 * B + (chunk + 1) * CHUNK)
            pair = returned[q, m // 2, rows, :B], returned[q, m // 2, rows, B:]
            points.append(scaled(pair, outer(m, 1)) if m else pair)
        for d, pair in enumerate(eighths(points, 1)):
            pair = scaled(pair, (inner_ref[d, 0, here, :], inner_ref[d, 1, here, :]))
            for part, value in enumerate(pair):
                high, low = split(value)
                at = part * B + chunk * CHUNK
                last[q, d // 2, at : at + CHUNK, lanes_of(d)] = high
                last[q, d // 2, 2 * B + at : 2 * B + at + CHUNK, lanes_of(d)] = low

    def fourth(q, pair_at):
        high, low = last[q, pair_at, : 2 * B], last[q, pair_at, 2 * B :]
        top = left_back_ref[:, : 2 * B]
        result = (
            jnp.dot(top, high, preferred_element_type=f32)
            + jnp.dot(left_back_ref[:, 2 * B :], high, preferred_element_type=f32)
            + jnp.dot(top, low, preferred_element_type=f32)
        )
        for d in (2 * pair_at, 2 * pair_at + 1):
            out_ref[pl.ds(8 * q + d, B, stride=16), :] = result[:, lanes_of(d)]

    def every(run, q, needs, count=PAIRS):
        return [((run.__name__, q, at), needs(at), lambda at=at: run(q, at)) for at in range(count)]

    def firsts(q):
        return every(first, q, lambda at: [("enter", q, 2 * at), ("enter", q, 2 * at + 1)])

    def seconds(q):
        return every(second, q, lambda at: [("middle", q, chunk) for chunk in range(CHUNKS)])

    def thirds(q):
        return every(third, q, lambda at: [("second", 2, at), ("second", 1 - q, at)])

    def fourths(q):
        return every(fourth, q, lambda at: [("middle_back", q, chunk) for chunk in range(CHUNKS)])

    def enters(q):
        return every(enter, q, lambda at: [], RADIX)

    def middles(q):
        return every(middle, q, lambda at: [("first", q, pair_at) for pair_at in range(PAIRS)], CHUNKS)

    def middles_back(q):
        return every(middle_back, q, lambda at: [("third", q, pair_at) for pair_at in range(PAIRS)], CHUNKS)

    tasks = firsts(2) + firsts(0) + seconds(2) + firsts(1) + seconds(0) + thirds(1)
    tasks += seconds(1) + thirds(0) + fourths(1) + fourths(0)
    fillers = enters(2) + enters(0) + middles(2) + enters(1) + middles(0) + middles(1)
    fillers += middles_back(1) + middles_back(0)
    interleaved(tasks, fillers)


def call(kernel, out_shape, in_spaces, out_spaces, name, scratch, interpret):
    return pl.pallas_call(
        kernel,
        out_shape=out_shape,
        in_specs=[pl.BlockSpec(memory_space=space) for space in in_spaces],
        out_specs=[pl.BlockSpec(memory_space=space) for space in out_spaces],
        scratch_shapes=scratch,
        name=name,
        interpret=interpret,
        compiler_params=pltpu.CompilerParams(vmem_limit_bytes=48 * 1024 * 1024),
    )


def pack(signal, filter_taps, grad_out, interpret=False):
    rows = signal.shape[0]
    shape = jax.ShapeDtypeStruct((24 * B, B), f32)
    scratch = [pltpu.VMEM((3, rows, B), f32), pltpu.SemaphoreType.DMA((3,))]
    packed = call(pack_kernel, [shape], [pltpu.HBM] * 3, [pltpu.VMEM], "pack", scratch, interpret)
    inputs = (signal, filter_taps, grad_out)
    if not interpret:
        inputs = [pltpu.with_memory_space_constraint(x, pltpu.HBM) for x in inputs]
    return packed(*inputs)[0].reshape(B, 24, B)


def transform(received, interpret=False):
    blocks = received.shape[0]
    length = blocks * 8 * B
    packed, inner, outer = tables(length)
    constants = [jnp.asarray(table) for table in packed] + [jnp.asarray(inner), jnp.asarray(outer)]

    shape = jax.ShapeDtypeStruct((blocks * 16, B), f32)
    scratch = [
        pltpu.VMEM((3, PAIRS, 2 * B, 2 * B), bf16),
        pltpu.VMEM((3, PAIRS, 2 * B, 2 * B), f32),
        pltpu.VMEM((3, RADIX * B, 2 * B), bf16),
        pltpu.VMEM((3, RADIX * B, 2 * B), bf16),
        pltpu.VMEM((2, PAIRS, 2 * B, 2 * B), f32),
        pltpu.VMEM((2, PAIRS, 4 * B, 2 * B), bf16),
    ]
    run = call(channel_kernel, [shape], [pltpu.VMEM] * 7, [pltpu.VMEM], "channel", scratch, interpret)
    return run(received.reshape(blocks * 24, B), *constants)[0].reshape(blocks, 16, B)


def unpack(received, interpret=False):
    rows = 8 * B
    shape = jax.ShapeDtypeStruct((rows, B), f32)
    scratch = [pltpu.VMEM((2, rows, B), f32), pltpu.SemaphoreType.DMA((2, rows // B))]
    return call(unpack_kernel, [shape] * 2, [pltpu.VMEM], [pltpu.HBM] * 2, "unpack", scratch, interpret)(received.reshape(16 * B, B))


def exchange(array):
    return lax.all_to_all(array, AXES, split_axis=0, concat_axis=0, tiled=True)


def shards(signal, filter_taps, grad_out):
    received = exchange(pack(signal, filter_taps, grad_out))
    returned = exchange(transform(received))
    first, second = unpack(returned)
    return first, second


def solution(mesh):
    return jax.shard_map(
        shards,
        mesh=mesh,
        in_specs=(P(AXES, None), P(AXES, None), P(AXES, None)),
        out_specs=(P(AXES, None), P(AXES, None)),
        check_vma=False,
    )
```

time: 68.2 us -> 68.3 us (level)
  no operation moved by 1% of the time
where the time goes in v4:
time: 68.3 us; the launch traced here: 68.1 us
  blocking collectives  58.5 us (86%)
  Pallas kernels  8.87 us (13%)
  between operations  0.72 us (1%)
    all_to_all x2, blocking collectives, exchange(): return lax.all_to_all(array, AXES, split_axis=0, concat_axis=0, tiled=True)  58.5 us
    pallas_call x1, Pallas kernels, transform(): run(received.reshape(blocks * 24, B), *constants)[0].reshape(blocks, 16, B)  6 us
    pallas_call x1, Pallas kernels, pack(): return packed(*inputs)[0].reshape(B, 24, B)  1.68 us

profile of v4, /device:TPU:0, one launch (start us, length us, event | category | flops | bytes accessed | tf_op | source)
XLA Modules:
  0.0 68.1 jit_solution(12664096251522233923)
XLA Ops:
  0.6 1.7 %pack.1 = f32[3072,128]{1,0:T(8,128)S(1)} custom-call(f32[1024,128]{1,0:T(8,128)} %signal_ref.1, f32[1024,128]{1,0:T(8,128)} %filter_ref.1, f32[1024,128]{1,0:T(8,128)} %grad_ref.1), custom_call_target="tpu_custom_call" | custom-call | tf_op jit(solution)/shard_map/pack/pallas_call | solution.py:253
  2.3 0.0 copy-start
  2.3 0.0 copy-start.1
  2.3 0.0 copy-start.2
  2.4 0.0 copy-start.3
  2.4 0.0 copy-start.4
  2.4 0.0 copy-start.5
  2.4 35.4 %all_to_all.10 = f32[128,24,128]{2,1,0:T(8,128)S(1)} all-to-all(f32[128,24,128]{2,1,0:T(8,128)S(1)} %bitcast.5), channel_id=1, replica_groups=mesh['gx'=16,'gy'=8] {'gx','gy'}, dimensions={0} | all-to-all | bytes 3145728 | tf_op jit(solution)/shard_map/all_to_all | solution.py:283
  37.8 0.0 copy-done
  37.8 0.0 copy-done.1
  37.8 0.0 copy-done.2
  37.8 0.0 copy-done.3
  37.8 0.0 copy-done.4
  37.8 0.0 copy-done.5
  37.8 6.0 %channel.1 = f32[2048,128]{1,0:T(8,128)S(1)} custom-call(f32[3072,128]{1,0:T(8,128)S(1)} %bitcast.4, bf16[256,384]{1,0:T(8,128)(2,1)S(1)} %copy-done.3, bf16[128,512]{1,0:T(8,128)(2,1)S(1)} %copy-done.4, bf16[512,256]{1,0:T(8,128)(2,1)S(1)} %copy-done.2, bf16[512,256]{1,0:T(8,128)(2,1)S(1)} %copy-done.1, f32[8,2,128,128]{3,2,1,0:T(8,128)S(1)} %copy-done, ...), custom_call_target="tpu_custom_call" | custom-call | tf_op jit(solution)/shard_map/channel/pallas_call | solution.py:272
  43.8 23.1 %all_to_all.11 = f32[128,16,128]{2,1,0:T(8,128)S(1)} all-to-all(f32[128,16,128]{2,1,0:T(8,128)S(1)} %bitcast.6), channel_id=1, replica_groups=mesh['gx'=16,'gy'=8] {'gx','gy'}, dimensions={0} | all-to-all | bytes 2097152 | tf_op jit(solution)/shard_map/all_to_all | solution.py:283
  66.9 1.2 %unpack.1 = (f32[1024,128]{1,0:T(8,128)}, f32[1024,128]{1,0:T(8,128)}) custom-call(f32[2048,128]{1,0:T(8,128)S(1)} %bitcast.7), custom_call_target="tpu_custom_call" | custom-call | tf_op jit(solution)/shard_map/unpack/pallas_call | solution.py:279
Async XLA Ops:
  2.3 35.5 %copy-start = (f32[8,2,128,128]{3,2,1,0:T(8,128)S(1)}, f32[8,2,128,128]{3,2,1,0:T(8,128)}, u32[]{:S(2)}) copy-start(f32[8,2,128,128]{3,2,1,0:T(8,128)} %constant.16.clone.inner_ref) | copy-start | bytes 3145732
  2.3 35.4 %copy-start.1 = (bf16[512,256]{1,0:T(8,128)(2,1)S(1)}, bf16[512,256]{1,0:T(8,128)(2,1)}, u32[]{:S(2)}) copy-start(bf16[512,256]{1,0:T(8,128)(2,1)} %constant.15.clone.right_back_ref) | copy-start | bytes 786436
  2.3 35.4 %copy-start.2 = (bf16[512,256]{1,0:T(8,128)(2,1)S(1)}, bf16[512,256]{1,0:T(8,128)(2,1)}, u32[]{:S(2)}) copy-start(bf16[512,256]{1,0:T(8,128)(2,1)} %constant.14.clone.right_ref) | copy-start | bytes 786436
  2.4 35.4 %copy-start.3 = (bf16[256,384]{1,0:T(8,128)(2,1)S(1)}, bf16[256,384]{1,0:T(8,128)(2,1)}, u32[]{:S(2)}) copy-start(bf16[256,384]{1,0:T(8,128)(2,1)} %constant.12.clone.left_ref) | copy-start | bytes 589828
  2.4 35.4 %copy-start.4 = (bf16[128,512]{1,0:T(8,128)(2,1)S(1)}, bf16[128,512]{1,0:T(8,128)(2,1)}, u32[]{:S(2)}) copy-start(bf16[128,512]{1,0:T(8,128)(2,1)} %constant.13.clone.left_back_ref) | copy-start | bytes 393220
  2.4 35.4 %copy-start.5 = (f32[16,128]{1,0:T(8,128)S(1)}, f32[16,128]{1,0:T(8,128)}, u32[]{:S(2)}) copy-start(f32[16,128]{1,0:T(8,128)} %constant.17.clone.outer_ref) | copy-start | bytes 24580

commit v5 on v3

--- a/solution.py
+++ b/solution.py
@@ -119,13 +119,17 @@
 
 
 def pack_kernel(signal_ref, filter_ref, grad_ref, out_ref, held, arrived):
+    rows = signal_ref.shape[0]
+    parts = [(0, 0, rows), (1, 0, rows), (2, 0, rows // 2), (2, rows // 2, rows // 2)]
     copies = []
-    for q, ref in enumerate((signal_ref, filter_ref, grad_ref)):
-        copies.append(pltpu.make_async_copy(ref, held.at[q], arrived.at[q]))
+    for n, (q, at, size) in enumerate(parts):
+        here = pl.ds(at, size)
+        ref = (signal_ref, filter_ref, grad_ref)[q]
+        copies.append(pltpu.make_async_copy(ref.at[here], held.at[q, here], arrived.at[n]))
         copies[-1].start()
-    for q, copy in enumerate(copies):
+    for copy, (q, at, size) in zip(copies, parts):
         copy.wait()
-        for r in range(8):
+        for r in range(at // B, (at + size) // B):
             out_ref[pl.ds(8 * q + r, B, stride=24), :] = held[q, r * B : (r + 1) * B, :].T
 
 
@@ -257,7 +261,7 @@
 def pack(signal, filter_taps, grad_out, interpret=False):
     rows = signal.shape[0]
     shape = jax.ShapeDtypeStruct((24 * B, B), f32)
-    scratch = [pltpu.VMEM((3, rows, B), f32), pltpu.SemaphoreType.DMA((3,))]
+    scratch = [pltpu.VMEM((3, rows, B), f32), pltpu.SemaphoreType.DMA((4,))]
     packed = call(pack_kernel, [shape], [pltpu.HBM] * 3, [pltpu.VMEM], "pack", scratch, interpret)
     inputs = (signal, filter_taps, grad_out)
     if not interpret:

time: 68.2 us -> 68.3 us (level)
  no operation moved by 1% of the time
where the time goes in v5:
time: 68.3 us; the launch traced here: 68.1 us
  blocking collectives  58.5 us (86%)
  Pallas kernels  8.88 us (13%)
  between operations  0.72 us (1%)
    all_to_all x2, blocking collectives, exchange(): return lax.all_to_all(array, AXES, split_axis=0, concat_axis=0, tiled=True)  58.5 us
    pallas_call x1, Pallas kernels, transform(): call(channel_kernel, [shape], [pltpu.VMEM] * 7, [pltpu.VMEM], 'channel',...  5.94 us
    pallas_call x1, Pallas kernels, pack(): return packed(*inputs)[0].reshape(B, 24, B)  1.75 us

profile of v5, /device:TPU:0, one launch (start us, length us, event | category | flops | bytes accessed | tf_op | source)
XLA Modules:
  0.0 68.1 jit_solution(15742338108691433777)
XLA Ops:
  0.6 1.8 %pack.1 = f32[3072,128]{1,0:T(8,128)S(1)} custom-call(f32[1024,128]{1,0:T(8,128)} %signal_ref.1, f32[1024,128]{1,0:T(8,128)} %filter_ref.1, f32[1024,128]{1,0:T(8,128)} %grad_ref.1), custom_call_target="tpu_custom_call" | custom-call | tf_op jit(solution)/shard_map/pack/pallas_call | solution.py:269
  2.4 0.0 copy-start
  2.4 0.0 copy-start.1
  2.4 0.0 copy-start.2
  2.4 0.0 copy-start.3
  2.4 0.0 copy-start.4
  2.5 0.0 copy-start.5
  2.5 35.4 %all_to_all.10.in_ref = f32[128,24,128]{2,1,0:T(8,128)S(1)} all-to-all(f32[128,24,128]{2,1,0:T(8,128)S(1)} %bitcast.2), channel_id=1, replica_groups=mesh['gx'=16,'gy'=8] {'gx','gy'}, dimensions={0} | all-to-all | bytes 3145728 | tf_op jit(solution)/shard_map/all_to_all | solution.py:291
  37.8 0.0 copy-done
  37.8 0.0 copy-done.1
  37.8 0.0 copy-done.2
  37.9 0.0 copy-done.3
  37.9 0.0 copy-done.4
  37.9 0.0 copy-done.5
  37.9 5.9 %channel.1 = f32[128,16,128]{2,1,0:T(8,128)S(1)} custom-call(f32[128,24,128]{2,1,0:T(8,128)S(1)} %all_to_all.10.in_ref, bf16[256,512]{1,0:T(8,128)(2,1)S(1)} %copy-done.4, bf16[256,512]{1,0:T(8,128)(2,1)S(1)} %copy-done.3, bf16[512,256]{1,0:T(8,128)(2,1)S(1)} %copy-done.2, bf16[512,256]{1,0:T(8,128)(2,1)S(1)} %copy-done.1, f32[8,2,128,128]{3,2,1,0:T(8,128)S(1)} %copy-done, ...), custom_call_target="tpu_custom_call" | custom-call | tf_op jit(solution)/shard_map/channel/pallas_call | solution.py:280
  43.8 23.1 %all_to_all.11 = f32[128,16,128]{2,1,0:T(8,128)S(1)} all-to-all(f32[128,16,128]{2,1,0:T(8,128)S(1)} %channel.1), channel_id=1, replica_groups=mesh['gx'=16,'gy'=8] {'gx','gy'}, dimensions={0} | all-to-all | bytes 2097152 | tf_op jit(solution)/shard_map/all_to_all | solution.py:291
  66.9 1.2 %unpack.1 = (f32[1024,128]{1,0:T(8,128)}, f32[1024,128]{1,0:T(8,128)}) custom-call(f32[2048,128]{1,0:T(8,128)S(1)} %bitcast.3), custom_call_target="tpu_custom_call" | custom-call | tf_op jit(solution)/shard_map/unpack/pallas_call | solution.py:287
Async XLA Ops:
  2.4 35.5 %copy-start = (f32[8,2,128,128]{3,2,1,0:T(8,128)S(1)}, f32[8,2,128,128]{3,2,1,0:T(8,128)}, u32[]{:S(2)}) copy-start(f32[8,2,128,128]{3,2,1,0:T(8,128)} %constant.16.clone.inner_ref) | copy-start | bytes 3145732
  2.4 35.4 %copy-start.1 = (bf16[512,256]{1,0:T(8,128)(2,1)S(1)}, bf16[512,256]{1,0:T(8,128)(2,1)}, u32[]{:S(2)}) copy-start(bf16[512,256]{1,0:T(8,128)(2,1)} %constant.15.clone.right_back_ref) | copy-start | bytes 786436
  2.4 35.4 %copy-start.2 = (bf16[512,256]{1,0:T(8,128)(2,1)S(1)}, bf16[512,256]{1,0:T(8,128)(2,1)}, u32[]{:S(2)}) copy-start(bf16[512,256]{1,0:T(8,128)(2,1)} %constant.14.clone.right_ref) | copy-start | bytes 786436
  2.4 35.4 %copy-start.3 = (bf16[256,512]{1,0:T(8,128)(2,1)S(1)}, bf16[256,512]{1,0:T(8,128)(2,1)}, u32[]{:S(2)}) copy-start(bf16[256,512]{1,0:T(8,128)(2,1)} %constant.13.clone.left_back_ref) | copy-start | bytes 786436
  2.4 35.4 %copy-start.4 = (bf16[256,512]{1,0:T(8,128)(2,1)S(1)}, bf16[256,512]{1,0:T(8,128)(2,1)}, u32[]{:S(2)}) copy-start(bf16[256,512]{1,0:T(8,128)(2,1)} %constant.12.clone.left_ref) | copy-start | bytes 786436
  2.5 35.4 %copy-start.5 = (f32[2,128,128]{2,1,0:T(8,128)S(1)}, f32[2,128,128]{2,1,0:T(8,128)}, u32[]{:S(2)}) copy-start(f32[2,128,128]{2,1,0:T(8,128)} %constant.17.clone.outer_ref) | copy-start | bytes 393220
